TPU v7x, 256 devices: a whole 4x4x8 slice. The times are simulated.
256 devices in a mesh: gx: 8 (over x, core), gy: 4 (over y), gz: 8 (over z).
Axes of the slice: x: 4, y: 4, z: 8, core: 2. Of those that a mesh axis runs over, the one named last changes fastest.
Arguments:
- query: bfloat16 [4, 4, 4096], replicated, may hold values from -50 to 50
- keys: bfloat16 [32768, 4, 4096], P(('gx', 'gy', 'gz')), may hold values from -6 to 6
- values: bfloat16 [32768, 4, 4096], P(('gx', 'gy', 'gz')), may hold values from -6 to 6
- lm_keys: bfloat16 [1024, 4, 4096], P(('gx', 'gy', 'gz')), may hold values from -10 to 10
- lm_values: bfloat16 [1024, 4, 4096], P(('gx', 'gy', 'gz')), may hold values from -6 to 6
- selected: int32 [4, 16, 16], replicated, may hold values from 0 to 1023, as said below
Outputs:
- attended: float32 [4, 4, 4096], P(None, None, ('gx', 'gy', 'gz'))
Inputs may be any that keep to these rules, and one draw needn't show every extreme that they name: `selected`: each batch row and head names 16 different blocks; every shard holds either none of them or exactly 2.
All inputs are finite; a program needn't handle non-finite values.
Results may differ from a plain program's by a relative error of at most 0.0007.
Values sent between devices are 32-bit elements; how exact they have to be, the bound alone decides.
No kernel may reach another device: no remote copies, remote signals or barrier semaphores. Data moves between devices by JAX's collectives and lax.ppermute only.
A program may use at most 64 MiB of HBM per device.

v0:
```python
import math

import jax
import jax.numpy as jnp
from jax import lax
from jax.sharding import Mesh
from jax.sharding import PartitionSpec as P

GX_GY_GZ = ("gx_0", "gx_1", "gy", "gz")


def combined_by_axis(x, axes, combine):
    for axis in axes:
        pieces = jax.tree.map(lambda part: lax.all_gather(part, axis), x)
        x = jax.tree.map(lambda part: part[0], pieces)
        for k in range(1, lax.axis_size(axis)):
            x = combine(x, jax.tree.map(lambda part: part[k], pieces))
    return x


def merge_parts(first, second):
    joint_peak = jnp.maximum(first[0], second[0])
    left_factor = jnp.exp(first[0] - joint_peak)
    right_factor = jnp.exp(second[0] - joint_peak)
    joint_total = first[1] * left_factor + second[1] * right_factor
    joint_sum = first[2] * left_factor[..., None] + second[2] * right_factor[..., None]
    return (joint_peak, joint_total, joint_sum)


def body(query, keys, values, lm_keys, lm_values, selected):
    device_count = lax.axis_size(GX_GY_GZ)
    my_index = lax.axis_index(GX_GY_GZ)
    positions, batch_rows, feature_width = keys.shape
    local_blocks = lm_keys.shape[0]
    block_len = positions // local_blocks
    head_count = selected.shape[1]
    head_width = feature_width // head_count
    draft_count = query.shape[1]
    query_heads = query.reshape(batch_rows, draft_count, head_count, head_width)
    score_scale = 1.0 / math.sqrt(head_width)
    block_ids = my_index * local_blocks + jnp.arange(local_blocks, dtype=jnp.int32)
    chosen_here = jnp.any(selected[:, :, :, None] == block_ids[None, None, None, :], axis=2)
    summary_keys = lm_keys.reshape(local_blocks, batch_rows, head_count, head_width)
    summary_values = lm_values.reshape(local_blocks, batch_rows, head_count, head_width)
    summary_score = (
        jnp.einsum("bphd,lbhd->bphl", query_heads, summary_keys, preferred_element_type=jnp.float32)
        * score_scale
    )
    keys_heads = keys.reshape(positions, batch_rows, head_count, head_width)
    values_heads = values.reshape(positions, batch_rows, head_count, head_width)
    live_tokens = jnp.repeat(chosen_here, block_len, axis=2)
    token_score = (
        jnp.einsum("bphd,tbhd->bpht", query_heads, keys_heads, preferred_element_type=jnp.float32)
        * score_scale
    )
    token_score = jnp.where(live_tokens[:, None], token_score, -jnp.inf)
    local_peak = jnp.maximum(jnp.max(token_score, -1), jnp.max(summary_score, -1))
    token_weight = jnp.exp(token_score - local_peak[..., None])
    summary_weight = jnp.exp(summary_score - local_peak[..., None])
    local_total = jnp.sum(token_weight, -1) + jnp.sum(summary_weight, -1)
    local_sum = jnp.einsum(
        "bpht,tbhd->bphd",
        token_weight.astype(jnp.bfloat16),
        values_heads,
        preferred_element_type=jnp.float32,
    ) + jnp.einsum(
        "bphl,lbhd->bphd",
        summary_weight.astype(jnp.bfloat16),
        summary_values,
        preferred_element_type=jnp.float32,
    )
    column_count = feature_width // device_count
    global_peak, denominator, numerator = combined_by_axis(
        (local_peak, local_total, local_sum), GX_GY_GZ, merge_parts
    )
    own_numerator = lax.dynamic_slice_in_dim(
        numerator.reshape(batch_rows, draft_count, feature_width),
        my_index * column_count,
        column_count,
        2,
    )
    spread_denominator = jnp.repeat(denominator, head_width, axis=2)
    own_denominator = lax.dynamic_slice_in_dim(
        spread_denominator, my_index * column_count, column_count, 2
    )
    return own_numerator / own_denominator


def solution(mesh):
    torus = Mesh(
        mesh.devices.reshape(4, 2, mesh.shape["gy"], mesh.shape["gz"]), ("gx_0", "gx_1", "gy", "gz")
    )
    in_specs = (
        P(),
        P(GX_GY_GZ, None, None),
        P(GX_GY_GZ, None, None),
        P(GX_GY_GZ, None, None),
        P(GX_GY_GZ, None, None),
        P(),
    )
    out_specs = P(None, None, GX_GY_GZ)
    return jax.shard_map(body, mesh=torus, in_specs=in_specs, out_specs=out_specs, check_vma=False)
```

profile of v0, /device:TPU:2, one launch (start us, length us, event | category | flops | bytes accessed | tf_op | source)
XLA Modules:
  0.0 185.3 jit_solution(9675996966107307699)
XLA Ops:
  6.5 1.2 compare_reduce_fusion
  7.9 0.1 broadcast_in_dim.18
  8.2 7.7 %reshape.548 = bf16[128,4,16,256]{3,2,1,0:T(8,128)(2,1)} reshape(bf16[128,4,4096]{2,1,0:T(4,128)(2,1)} %param.7) | data formatting | bytes 8388608 | tf_op jit(solution)/shard_map/reshape | solution.py:49
  16.0 7.8 %reshape.551 = bf16[128,4,16,256]{3,2,1,0:T(8,128)(2,1)} reshape(bf16[128,4,4096]{2,1,0:T(4,128)(2,1)} %param.8) | data formatting | bytes 8388608 | tf_op jit(solution)/shard_map/reshape | solution.py:50
  23.9 0.2 fusion.109
  24.1 4.8 %fusion.108 = (f32[4,4,16]{1,2,0:T(8,128)S(1)}, f32[4,4,16,128]{3,1,2,0:T(4,128)S(1)}) fusion(bf16[4,4,16,256]{3,1,2,0:T(4,128)(2,1)S(1)} %bitcast.382, bf16[128,4,16,256]{3,2,1,0:T(8,128)(2,1)} %reshape.548, pred[4,16,128]{2,1,0:T(8,128)(4,1)S(1)} %broadcast_in_dim.19), kind=kOutput, calls=%fused_computation.188 | convolution fusion | flops 16875264 | bytes 4465664 | tf_op jit(solution)/shard_map/bphd,tbhd->bpht/dot_general | solution.py:53
  28.9 2.4 %fusion = f32[4,16,4,256]{3,2,1,0:T(4,128)S(1)} fusion(bf16[128,4,16,256]{3,2,1,0:T(8,128)(2,1)S(1)} %copy-done.1, f32[4,4,16,128]{3,1,2,0:T(4,128)S(1)} %get-tuple-element.54, f32[4,4,16]{1,2,0:T(8,128)S(1)} %max.347), kind=kOutput, calls=%fused_computation | convolution fusion | flops 16842752 | bytes 4588544 | tf_op jit(solution)/shard_map/bpht,tbhd->bphd/dot_general | solution.py:61
  31.3 0.3 fusion.4
  31.6 0.8 copy.57
  32.6 0.3 fusion.32
  33.0 12.0 %all-gather.1 = f32[16,4,16]{2,1,0:T(4,128)S(1)} all-gather(f32[4,4,16]{2,1,0:T(4,128)S(1)} %copy.58), channel_id=3, replica_groups=mesh['gx_0'=4,'gx_1'=2,'gy'=4,'gz'=8] {'gx_0'}, dimensions={0}, use_global_device_ids=true | all-gather | bytes 5120 | tf_op jit(solution)/shard_map/all_gather | solution.py:14
  45.0 11.9 %all-gather.2 = f32[16,4,16]{2,1,0:T(4,128)S(1)} all-gather(f32[4,4,16]{2,1,0:T(4,128)S(1)} %copy.59), channel_id=4, replica_groups=mesh['gx_0'=4,'gx_1'=2,'gy'=4,'gz'=8] {'gx_0'}, dimensions={0}, use_global_device_ids=true | all-gather | bytes 5120 | tf_op jit(solution)/shard_map/all_gather | solution.py:14
  56.9 1.8 all_gather.54
  58.8 2.1 %all-gather.11.cloned.1.call-done = f32[16,4,16,256]{3,2,1,0:T(8,128)} async-done(((f32[4,4,16,256]{3,2,1,0:T(8,128)}), f32[16,4,16,256]{3,2,1,0:T(8,128)}) %all-gather.11.cloned.1.call-update) | async-done | bytes 1048592 | tf_op jit(solution)/shard_map/all_gather | solution.py:14
  60.9 1.5 fusion.22
  62.4 2.2 %all_gather.53 = f32[2,4,4,16,256]{4,3,2,1,0:T(8,128)S(1)} all-gather(f32[1,4,4,16,256]{4,3,2,1,0:T(8,128)S(1)} %fusion.22), channel_id=1, replica_groups=mesh['gx_0'=4,'gx_1'=2,'gy'=4,'gz'=8] {'gx_1'}, dimensions={0}, use_global_device_ids=true | all-gather | bytes 786432 | tf_op jit(solution)/shard_map/all_gather | solution.py:14
  64.6 0.8 fusion.20
  65.5 1.8 all_gather.60
  67.3 12.3 %all_gather.56 = f32[4,4,4,16]{3,2,1,0:T(4,128)S(1)} all-gather(f32[1,4,4,16]{3,2,1,0:T(4,128)S(1)} %get-tuple-element.23), channel_id=1, replica_groups=mesh['gx_0'=4,'gx_1'=2,'gy'=4,'gz'=8] {'gy'}, dimensions={0}, use_global_device_ids=true | all-gather | bytes 5120 | tf_op jit(solution)/shard_map/all_gather | solution.py:14
  79.7 14.2 %all-gather.7.cloned.1.call-done = f32[4,4,4,16,256]{4,3,2,1,0:T(8,128)} async-done(((f32[1,4,4,16,256]{4,3,2,1,0:T(8,128)}), f32[4,4,4,16,256]{4,3,2,1,0:T(8,128)}) %all-gather.7.cloned.1.call-update) | async-done | bytes 1048592 | tf_op jit(solution)/shard_map/all_gather | solution.py:14
  93.9 2.2 %fusion.15 = f32[1,4,4,16,256]{4,3,2,1,0:T(8,128)} fusion(f32[4,4,4,16,256]{4,3,2,1,0:T(8,128)} %all-gather.7.cloned.1.call-done, f32[4,4,16]{2,1,0:T(4,128)S(1)} %get-tuple-element.45, f32[4,4,16]{2,1,0:T(4,128)S(1)} %get-tuple-element.42, f32[4,4,16]{2,1,0:T(4,128)S(1)} %get-tuple-element.44, f32[4,4,16]{2,1,0:T(4,128)S(1)} %get-tuple-element.43, ...), kind=kLoop, calls=%fused_computation.12 | loop fusion | flops 589824 | bytes 1316864 | tf_op jit(solution)/shard_map/add | solution.py:26
  96.1 11.9 %all_gather.61 = f32[4,4,4,16]{3,2,1,0:T(4,128)S(1)} all-gather(f32[1,4,4,16]{3,2,1,0:T(4,128)S(1)} %get-tuple-element.22), channel_id=1, replica_groups=mesh['gx_0'=4,'gx_1'=2,'gy'=4,'gz'=8] {'gy'}, dimensions={0}, use_global_device_ids=true | all-gather | bytes 5120 | tf_op jit(solution)/shard_map/all_gather | solution.py:14
  108.0 26.2 %all_gather.58 = f32[8,4,4,16]{3,2,1,0:T(4,128)S(1)} all-gather(f32[1,4,4,16]{3,2,1,0:T(4,128)S(1)} %get-tuple-element.21), channel_id=1, replica_groups=mesh['gx_0'=4,'gx_1'=2,'gy'=4,'gz'=8] {'gz'}, dimensions={0}, use_global_device_ids=true | all-gather | bytes 9216 | tf_op jit(solution)/shard_map/all_gather | solution.py:14
  134.2 24.8 %all_gather.62 = f32[8,4,4,16]{3,2,1,0:T(4,128)S(1)} all-gather(f32[1,4,4,16]{3,2,1,0:T(4,128)S(1)} %get-tuple-element.20), channel_id=1, replica_groups=mesh['gx_0'=4,'gx_1'=2,'gy'=4,'gz'=8] {'gz'}, dimensions={0}, use_global_device_ids=true | all-gather | bytes 9216 | tf_op jit(solution)/shard_map/all_gather | solution.py:14
  159.1 0.1 mul.469
  159.4 0.1 mul.466
  159.6 0.1 mul.463
  159.8 0.1 mul.460
  160.1 0.1 mul.457
  160.3 0.1 mul.454
  160.6 0.1 mul.451
  160.8 0.1 mul.448
  161.0 0.8 mul.472
  162.0 0.8 mul.475
  162.9 0.8 mul.478
  163.9 0.8 mul.481
  164.8 0.8 mul.484
  165.7 0.8 mul.487
  166.7 0.8 reshape.553
  167.5 2.6 %fusion.107 = (f32[1,4,4,16,256]{4,3,2,1,0:T(8,128)}, f32[1,4,4,16,256]{4,3,2,1,0:T(8,128)}, f32[1,4,4,16,256]{4,3,2,1,0:T(8,128)}, f32[1,4,4,16,256]{4,3,2,1,0:...) fusion(f32[8,4,4,16,256]{4,3,2,1,0:T(8,128)} %all-gather.9.clon, ...), kind=kLoop, calls=%fused_computation.187 | loop fusion | bytes 4194304 | tf_op jit(solution)/shard_map/slice | solution.py:15
  170.4 0.1 squeeze.137
  170.5 0.1 squeeze.135
  170.7 1.1 squeeze.132
  171.7 1.8 squeeze.143
  173.5 1.8 squeeze.145
  175.3 1.8 squeeze.147
  177.1 0.2 multiply_add_fusion
  177.2 1.6 fusion.85
  (52 shorter events, 2.7 us)
Async XLA Ops:
  6.5 17.3 %copy-start = (bf16[4,4,4096]{2,1,0:T(4,128)(2,1)S(1)}, bf16[4,4,4096]{2,1,0:T(4,128)(2,1)}, u32[]{:S(2)}) copy-start(bf16[4,4,4096]{2,1,0:T(4,128)(2,1)} %param.6) | copy-start | bytes 393220
  6.5 54.4 %all-gather.11.cloned.1.call-start = ((), (), s32[]{:S(2)}) async-start(), calls=%async_computation.2 | async-start | bytes 1310720 | tf_op jit(solution)/shard_map/all_gather | solution.py:14
  8.1 7.7 %copy-start.2 = (bf16[4,4,4096]{2,1,0:T(4,128)(2,1)S(1)}, bf16[4,4,4096]{2,1,0:T(4,128)(2,1)}, u32[]{:S(2)}) copy-start(bf16[4,4,4096]{2,1,0:T(4,128)(2,1)} %param.9) | copy-start | bytes 393220
  16.0 7.8 %copy-start.3 = (bf16[4,4,4096]{2,1,0:T(4,128)(2,1)S(1)}, bf16[4,4,4096]{2,1,0:T(4,128)(2,1)}, u32[]{:S(2)}) copy-start(bf16[4,4,4096]{2,1,0:T(4,128)(2,1)} %param.10) | copy-start | bytes 393220
  23.9 5.1 %copy-start.1 = (bf16[128,4,16,256]{3,2,1,0:T(8,128)(2,1)S(1)}, bf16[128,4,16,256]{3,2,1,0:T(8,128)(2,1)}, u32[]{:S(2)}) copy-start(bf16[128,4,16,256]{3,2,1,0:T(8,128)(2,1)} %reshape.551) | copy-start | bytes 12582916
  32.4 61.5 %all-gather.7.cloned.1.call-start = ((), (), s32[]{:S(2)}) async-start(), calls=%async_computation | async-start | bytes 1310720 | tf_op jit(solution)/shard_map/all_gather | solution.py:14
  65.4 102.0 %all-gather.9.cloned.1.call-start = ((), (), s32[]{:S(2)}) async-start(), calls=%async_computation.1 | async-start | bytes 2359296 | tf_op jit(solution)/shard_map/all_gather | solution.py:14
Sparse Core Ops, SparseCore 0:
  32.5 28.4 all-gather.10
  65.6 28.2 all-gather.6
  96.2 41.3 all-gather.8
where the time goes:
time: 186 us; the launch traced here: 185 us
  blocking collectives  105 us (56%)
  local copies, waits for them, and re-layouts  34.8 us (19%)
  waiting for transfers between devices  16.4 us (9%)
  between operations  13.5 us (7%)
  other arithmetic  7.99 us (4%)
  matrix products  7.68 us (4%)
    all_gather x9, blocking collectives, combined_by_axis(): pieces = jax.tree.map(lambda part: lax.all_gather(part, axis), x)  105 us
    all_gather x3, waiting for transfers between devices, combined_by_axis(): pieces = jax.tree.map(lambda part: lax.all_gather(part, axis), x)  16.4 us
    reshape x1, local copies, waits for them, and re-layouts, body(): values_heads = values.reshape(positions, batch_rows, head_count, head_width)  7.79 us
    reshape x1, local copies, waits for them, and re-layouts, body(): keys_heads = keys.reshape(positions, batch_rows, head_count, head_width)  7.73 us
    squeeze x7, local copies, waits for them, and re-layouts, combined_by_axis(): x = combine(x, jax.tree.map(lambda part: part[k], pieces))  5.83 us
    dot_general x1, matrix products, body(): jnp.einsum('bphd,tbhd->bpht', query_heads, keys_heads, preferred_element_...  4.8 us
    add x4, other arithmetic, merge_parts(): first[2] * left_factor[..., None] + second[2] * right_factor[..., None]  4.61 us
  transfers between devices with their start and end apart: 3, of which 2 were waited for; matrix products, arithmetic and copies ran while one was open for 5% of the time, Pallas kernels for 0%

commit v1 on v0

v1 whole, which is shorter than its diff:
```python
import math

import jax
import jax.numpy as jnp
from jax import lax
from jax.experimental import pallas as pl
from jax.experimental.pallas import tpu as pltpu
from jax.sharding import Mesh
from jax.sharding import PartitionSpec as P

AXES = ("x", "core", "gy", "gz")
CHIP_AXES = ("x", "gy", "gz")
HEADS = 16
LANES = 128
NEG_INF = float("-inf")


def attend_kernel(
    query_ref, selected_ref, summary_key_ref, summary_value_ref, keys_hbm, values_hbm,
    keep_ref, send_ref, key_buf, value_buf, rows_ref, key_sems, value_sems,
):
    my_core = lax.axis_index("core")
    my_index = lax.axis_index(AXES)

    def head_of(slot):
        half, pos = slot // 8, slot % 8
        core = my_core if half == 0 else 1 - my_core
        return (pos // 2) * 4 + core * 2 + pos % 2

    order = [8 + i for i in range(8)] + list(range(8))

    def copies(hbm, buf, sems, slot):
        head = head_of(slot)
        return [
            pltpu.make_async_copy(hbm.at[:, 2 * head + i], buf.at[slot, i], sems.at[slot, i]) for i in range(2)
        ]

    for slot in order:
        for cp in copies(keys_hbm, key_buf, key_sems, slot):
            cp.start()
        for cp in copies(values_hbm, value_buf, value_sems, slot):
            cp.start()

    row = lax.broadcasted_iota(jnp.int32, (16, LANES), 0) // 4
    lane = lax.broadcasted_iota(jnp.int32, (16, LANES), 1)
    same_row = row == lane % 4
    same_row16 = same_row[:, :16]
    scale = 1.0 / math.sqrt(2 * LANES)
    nt = (((1,), (1,)), ((), ()))
    nn = (((1,), (0,)), ((), ()))

    def small(ref, head):
        parts = [ref[:, 2 * head + i].reshape(16, LANES) for i in range(2)]
        return jnp.concatenate(parts, axis=1)

    def big(buf, slot):
        parts = [buf.at[slot, i].reshape(512, LANES)[...] for i in range(2)]
        return jnp.concatenate(parts, axis=1)

    def scores(slot):
        head = head_of(slot)
        for cp in copies(keys_hbm, key_buf, key_sems, slot):
            cp.wait()
        q = small(query_ref, head)
        s = lax.dot_general(q, big(key_buf, slot), nt, preferred_element_type=jnp.float32) * scale
        s2 = lax.dot_general(q, small(summary_key_ref, head), nt, preferred_element_type=jnp.float32) * scale
        chosen = selected_ref[head]
        tiles = []
        for blk in range(4):
            here = jnp.max(jnp.where(chosen == my_index * 4 + blk, 1.0, 0.0), axis=1, keepdims=True)
            ok = same_row & (here > 0.0)
            tiles.append(jnp.where(ok, s[:, blk * LANES:(blk + 1) * LANES], NEG_INF))
        return tiles, jnp.where(same_row16, s2, NEG_INF)

    def weights(tiles, s2):
        top = jnp.maximum(jnp.maximum(tiles[0], tiles[1]), jnp.maximum(tiles[2], tiles[3]))
        peak = jnp.maximum(jnp.max(top, axis=1, keepdims=True), jnp.max(s2, axis=1, keepdims=True))
        w = [jnp.exp(t - peak) for t in tiles]
        w2 = jnp.exp(s2 - peak)
        total = jnp.sum(w[0] + w[1] + (w[2] + w[3]), axis=1, keepdims=True) + jnp.sum(w2, axis=1, keepdims=True)
        return jnp.concatenate([t.astype(jnp.bfloat16) for t in w], axis=1), w2.astype(jnp.bfloat16), peak, total

    def weighted(slot, w, w2, peak, total):
        for cp in copies(values_hbm, value_buf, value_sems, slot):
            cp.wait()
        out = lax.dot_general(w, big(value_buf, slot), nn, preferred_element_type=jnp.float32)
        out = out + lax.dot_general(
            w2, small(summary_value_ref, head_of(slot)), nn, preferred_element_type=jnp.float32
        )
        half, pos = slot // 8, slot % 8
        for bp in range(16):
            rows_ref[half, 0, bp, pos:pos + 1, :] = out[bp:bp + 1, :LANES]
            rows_ref[half, 1, bp, pos:pos + 1, :] = out[bp:bp + 1, LANES:]
            rows_ref[half, 2, bp, pos:pos + 1, :] = jnp.broadcast_to(peak[bp:bp + 1], (1, LANES))
            rows_ref[half, 3, bp, pos:pos + 1, :] = jnp.broadcast_to(total[bp:bp + 1], (1, LANES))

    stage_a, stage_b = {}, {}
    for step in range(len(order) + 2):
        if step < len(order):
            stage_a[step] = scores(order[step])
        if 0 <= step - 1 < len(order):
            stage_b[step - 1] = weights(*stage_a.pop(step - 1))
        if 0 <= step - 2 < len(order):
            weighted(order[step - 2], *stage_b.pop(step - 2))

    lane8 = lax.broadcasted_iota(jnp.int32, (8, LANES), 1)
    for half, out_ref in ((0, keep_ref), (1, send_ref)):
        for hi in range(2):
            for tile in range(2):
                a = [rows_ref[half, tile, hi * 8 + i] for i in range(8)]
                for bit in range(3):
                    step = 1 << bit
                    width = 16 * step
                    upper = (lane8 // width) % 2 == 1
                    for i in range(8):
                        if i & step:
                            continue
                        u, v = a[i], a[i | step]
                        a[i] = jnp.where(upper, pltpu.roll(v, width, 1), u)
                        a[i | step] = jnp.where(upper, v, pltpu.roll(u, LANES - width, 1))
                for i in range(8):
                    out_ref[pl.ds((tile * 8 + i) * 3 + hi, 8, stride=48), :] = a[i]
        group, part = lane8 // 16, (lane8 % 16) // 4
        extra = jnp.zeros((8, LANES), jnp.float32)
        for what in range(4):
            for i in range(8):
                value = rows_ref[half, 2 + what // 2, (what % 2) * 8 + i]
                extra = jnp.where((group == i) & (part == what), value, extra)
        for d in range(16):
            out_ref[pl.ds(d * 3 + 2, 8, stride=48), :] = extra


def spread(x, lane, offset):
    if offset:
        x = jnp.where(lane % 8 < 4, pltpu.roll(x, LANES - 4, 1), x)
    else:
        x = jnp.where(lane % 8 < 4, x, pltpu.roll(x, 4, 1))
    return jnp.where(lane % 16 < 8, x, pltpu.roll(x, 8, 1))


def pair_kernel(first_ref, second_ref, out_ref):
    n = first_ref.shape[0] // 3
    lane = lax.broadcasted_iota(jnp.int32, (n, LANES), 1)
    e = [r[pl.ds(2, n, stride=3), :] for r in (first_ref, second_ref)]
    peak = jnp.maximum(e[0], e[1])
    f = [jnp.exp(t - peak) for t in e]
    total = sum(ft * pltpu.roll(t, LANES - 8, 1) for ft, t in zip(f, e))
    out_ref[pl.ds(2, n, stride=3), :] = jnp.where(lane % 16 < 8, peak, pltpu.roll(total, 8, 1))
    for hi in range(2):
        g = [spread(t, lane, 4 * hi) for t in f]
        out_ref[pl.ds(hi, n, stride=3), :] = (
            first_ref[pl.ds(hi, n, stride=3), :] * g[0] + second_ref[pl.ds(hi, n, stride=3), :] * g[1]
        )


def merge_kernel(parts_ref, out_ref):
    n = parts_ref.shape[0] // 3
    lane = lax.broadcasted_iota(jnp.int32, (n, LANES), 1)
    e = parts_ref[pl.ds(2, n, stride=3), :]
    f = jnp.exp(e - jnp.max(e, axis=0, keepdims=True))
    total = jnp.sum(f * pltpu.roll(e, LANES - 8, 1), axis=0, keepdims=True)
    for hi in range(2):
        g = spread(f, lane, 4 * hi)
        num = jnp.sum(parts_ref[pl.ds(hi, n, stride=3), :] * g, axis=0, keepdims=True)
        den = spread(jnp.broadcast_to(total, (8, LANES)), lane[:8], 4 * hi)
        res = jnp.broadcast_to(num, (8, LANES)) / den
        for i in range(8):
            row = hi * 8 + i
            out_ref[row // 4, row % 4:row % 4 + 1, :] = pltpu.roll(res, LANES - 16 * i, 1)[:1, :16] if i else res[:1, :16]


def body(query, keys, values, lm_keys, lm_values, selected):
    def tiled(a):
        lead, rows, width = a.shape
        return a.reshape(lead, rows, width // LANES, LANES).transpose(0, 2, 1, 3)

    vmem = pl.BlockSpec(memory_space=pltpu.VMEM)
    hbm = pl.BlockSpec(memory_space=pltpu.HBM)
    chosen = jnp.repeat(selected.transpose(1, 0, 2), query.shape[1], axis=1)
    state = jax.ShapeDtypeStruct((128 * 3, LANES), jnp.float32)
    keep, send = pl.pallas_call(
        attend_kernel,
        out_shape=(state, state),
        in_specs=[vmem, vmem, vmem, vmem, hbm, hbm],
        out_specs=(vmem, vmem),
        scratch_shapes=[
            pltpu.VMEM((HEADS, 2, 128, 4, LANES), jnp.bfloat16),
            pltpu.VMEM((HEADS, 2, 128, 4, LANES), jnp.bfloat16),
            pltpu.VMEM((2, 4, 16, 8, LANES), jnp.float32),
            pltpu.SemaphoreType.DMA((HEADS, 2)),
            pltpu.SemaphoreType.DMA((HEADS, 2)),
        ],
        compiler_params=pltpu.CompilerParams(vmem_limit_bytes=61 * 1024 * 1024),
        name="attend",
    )(tiled(query), chosen, tiled(lm_keys), tiled(lm_values), tiled(keys), tiled(values))
    other = lax.ppermute(send, "core", [(0, 1), (1, 0)])
    both = pl.pallas_call(
        pair_kernel, out_shape=state, in_specs=[vmem, vmem], out_specs=vmem, name="pair",
        compiler_params=pltpu.CompilerParams(vmem_limit_bytes=4 * 1024 * 1024),
    )(keep, other)
    parts = lax.all_to_all(both.reshape(128, 1, 3 * LANES), CHIP_AXES, 0, 0, tiled=True)
    return pl.pallas_call(
        merge_kernel,
        out_shape=jax.ShapeDtypeStruct((4, 4, 16), jnp.float32),
        in_specs=[vmem],
        out_specs=vmem,
        name="merge",
        compiler_params=pltpu.CompilerParams(vmem_limit_bytes=4 * 1024 * 1024),
    )(parts.reshape(128 * 3, LANES))


def solution(mesh):
    torus = Mesh(mesh.devices.reshape(4, 2, mesh.shape["gy"], mesh.shape["gz"]), AXES)
    split = P(AXES, None, None)
    return jax.shard_map(
        body,
        mesh=torus,
        in_specs=(P(), split, split, split, split, P()),
        out_specs=P(None, None, AXES),
        check_vma=False,
    )
```

time: 186 us -> 45 us (0.24)
  the two profiles are of different devices: /device:TPU:2 before, /device:TPU:1 now
where the time goes in v1:
time: 45 us; the launch traced here: 44.8 us
  blocking collectives  26.3 us (58%)
  Pallas kernels  11.5 us (26%)
  starting transfers between devices  3.29 us (7%)
  local copies, waits for them, and re-layouts  2.37 us (5%)
  waiting for transfers between devices  1.28 us (3%)
    all_to_all x1, blocking collectives, body(): lax.all_to_all(both.reshape(128, 1, 3 * LANES), CHIP_AXES, 0, 0, tiled=True)  26.3 us
    pallas_call x1, Pallas kernels, body(): pl.pallas_call(attend_kernel, out_shape=(state, state), in_specs=[vmem, v...  10.2 us
    ppermute x1, starting transfers between devices, body(): other = lax.ppermute(send, 'core', [(0, 1), (1, 0)])  3.29 us
    ppermute x1, waiting for transfers between devices, body(): other = lax.ppermute(send, 'core', [(0, 1), (1, 0)])  1.28 us
    unnamed x2, local copies, waits for them, and re-layouts  0.93 us
    pallas_call x1, Pallas kernels, body(): pl.pallas_call(merge_kernel, out_shape=jax.ShapeDtypeStruct((4, 4, 16), j...  0.91 us
  transfers between devices with their start and end apart: 1, of which 1 were waited for; matrix products, arithmetic and copies ran while one was open for 0% of the time, Pallas kernels for 0%

profile of v1, /device:TPU:1, one launch (start us, length us, event | category | flops | bytes accessed | tf_op | source)
XLA Modules:
  0.0 44.8 jit_solution(14739873848868964735)
XLA Ops:
  0.0 0.8 %copy.8 = s32[16,4,16]{2,1,0:T(4,128)S(1)} copy(s32[16,4,16]{2,0,1:T(8,128)} %bitcast.27) | data formatting | bytes 8192 | tf_op jit(solution)/shard_map/transpose | solution.py:179
  0.8 0.7 %broadcast_in_dim.3 = s32[16,4,4,16]{3,2,1,0:T(4,128)} broadcast(s32[16,4,16]{2,1,0:T(4,128)S(1)} %copy.8), dimensions={0,1,3} | broadcast | bytes 20480 | tf_op jit(solution)/shard_map/broadcast_in_dim | solution.py:179
  1.5 10.2 %attend.1 = (f32[384,128]{1,0:T(8,128)}, f32[384,128]{1,0:T(8,128)}) custom-call(bf16[4,32,4,128]{3,2,1,0:T(4,128)(2,1)} %bitcast.24, s32[16,16,16]{2,1,0:T(8,128)} %bitcast.23, bf16[4,32,4,128]{3,2,1,0:T(4,128)(2,1)} %bitcast.25, bf16[4,32,4,128]{3,2,1,0:T(4,128)(2,1)} %bitcast.26, bf16[128,32,4,128]{3,2,1,0:T(4,128)(2,1)} %bitcast.21, ...), custom_call_target="tpu_custom_call" | custom-call | tf_op jit(solution)/shard_map/attend/pallas_call | solution.py:181
  11.7 3.3 %collective-permute-start = (f32[384,128]{1,0:T(8,128)}, f32[384,128]{1,0:T(8,128)S(1)}, u32[]{:S(2)}, u32[]{:S(2)}) collective-permute-start(f32[384,128]{1,0:T(8,128)} %get-tuple-element.8), channel_id=1, source_target_pairs={{0,32},{32,0},{1,33},{33,1},{2,34},{34,2},{3,35},{35,3},{4,36},{36... | collective-permute-start | bytes 589832 | tf_op jit(solution)/shard_map/ppermute | solution.py:196
  15.0 1.3 %collective-permute-done.second_ref = f32[384,128]{1,0:T(8,128)S(1)} collective-permute-done((f32[384,128]{1,0:T(8,128)}, f32[384,128]{1,0:T(8,128)S(1)}, u32[]{:S(2)}, u32[]{:S(2)}) %collective-permute-start) | collective-permute-done | bytes 196640 | tf_op jit(solution)/shard_map/ppermute | solution.py:196
  16.3 0.0 copy-start
  16.3 0.9 %copy-done = f32[384,128]{1,0:T(8,128)S(1)} copy-done((f32[384,128]{1,0:T(8,128)S(1)}, f32[384,128]{1,0:T(8,128)}, u32[]{:S(2)}) %copy-start) | copy-done | bytes 196632
  17.2 0.4 pair.1
  17.6 26.3 %all_to_all.5 = f32[128,1,384]{2,1,0:T(1,128)S(1)} all-to-all(f32[128,1,384]{2,1,0:T(1,128)S(1)} %bitcast.20), channel_id=1, replica_groups=mesh['x'=4,'core'=2,'gy'=4,'gz'=8] {'x','gy','gz'}, dimensions={0} | all-to-all | bytes 393216 | tf_op jit(solution)/shard_map/all_to_all | solution.py:201
  43.9 0.9 %merge.1 = f32[4,4,16]{2,1,0:T(4,128)} custom-call(f32[384,128]{1,0:T(8,128)S(1)} %bitcast.19), custom_call_target="tpu_custom_call" | custom-call | tf_op jit(solution)/shard_map/merge/pallas_call | solution.py:202
Async XLA Ops:
  11.7 4.6 %collective-permute-start = (f32[384,128]{1,0:T(8,128)}, f32[384,128]{1,0:T(8,128)S(1)}, u32[]{:S(2)}, u32[]{:S(2)}) collective-permute-start(f32[384,128]{1,0:T(8,128)} %get-tuple-element.8), channel_id=1, source_target_pairs={{0,32},{32,0},{1,33},{33,1},{2,34},{34,2},{3,35},{35,3},{4,36},{36... | collective-permute-start | bytes 589832 | tf_op jit(solution)/shard_map/ppermute | solution.py:196
  16.3 0.9 %copy-start = (f32[384,128]{1,0:T(8,128)S(1)}, f32[384,128]{1,0:T(8,128)}, u32[]{:S(2)}) copy-start(f32[384,128]{1,0:T(8,128)} %get-tuple-element.7.first_ref) | copy-start | bytes 589828
